TPU v7x, 16 devices: a whole 2x2x2 slice. The times are simulated.
16 devices in a mesh: dp: 2 (over z), ep: 8 (over y, x, core).
Axes of the slice: x: 2, y: 2, z: 2, core: 2. Of those that a mesh axis runs over, the one named last changes fastest.
Arguments:
- x_in: bfloat16 [2048, 2304], P(('dp', 'ep')), parts along dimension 0
- topk_idx: int32 [2048, 2], P(('dp', 'ep')), parts along dimension 0
- topk_w: float32 [2048, 2], P(('dp', 'ep')), parts along dimension 0
- w_up: bfloat16 [8, 2304, 5760], P('ep')
- w_down: bfloat16 [8, 5760, 2304], P('ep')
Outputs:
- output: bfloat16 [2048, 2304], P(('dp', 'ep')), parts along dimension 0
There are 2 independent parts. A program takes and returns all parts, laid end to end along the dimension named above; an argument that names none is the same for every part.
All inputs are finite; a program needn't handle non-finite values.
Results may differ from a plain program's by a relative error of at most 0.001.
Values are sent between devices in bfloat16 or wider.
A program may use at most 1 GiB of HBM per device.

v0:
```python
import jax
import jax.numpy as jnp
from jax import lax
from jax.sharding import PartitionSpec as P


def slot_layout(expert_ids, num_experts, slot_cap):
    flat_ids = expert_ids.reshape(-1)
    expert_hits = (flat_ids[:, None] == jnp.arange(num_experts, dtype=jnp.int32)[None, :]).astype(jnp.int32)
    earlier = jnp.cumsum(expert_hits, axis=0) - expert_hits
    return flat_ids * slot_cap + jnp.sum(earlier * expert_hits, axis=1)


def solution(mesh):
    group = mesh.shape['ep']
    token_spec = P(('dp', 'ep'), None)
    expert_spec = P('ep', None, None)

    def local_layer(x_loc, ids_loc, gates_loc, w_up, w_down):
        tok_n, top_n = ids_loc.shape
        model_dim = x_loc.shape[1]
        local_experts = w_up.shape[0]
        num_experts = local_experts * group
        slot_cap = tok_n // 2
        slot_ids = slot_layout(ids_loc, num_experts, slot_cap)
        slot_range = jnp.arange(num_experts * slot_cap, dtype=jnp.int32)
        placed = jnp.any(slot_ids.reshape(tok_n, top_n, 1) == slot_range, axis=1).astype(jnp.bfloat16)
        send_rows = jnp.einsum('ts,tm->sm', placed, x_loc, preferred_element_type=jnp.float32).astype(jnp.bfloat16)
        send_rows = send_rows.reshape(group, local_experts, slot_cap, model_dim)
        recv_rows = lax.all_to_all(send_rows, 'ep', 0, 2, tiled=True)
        recv_rows = recv_rows.reshape(local_experts, group * slot_cap, model_dim)
        hidden = jnp.einsum('ecm,emf->ecf', recv_rows, w_up, preferred_element_type=jnp.float32)
        hidden = jax.nn.gelu(hidden, approximate=True).astype(jnp.bfloat16)
        expert_out = jnp.einsum('ecf,efm->ecm', hidden, w_down, preferred_element_type=jnp.float32).astype(jnp.bfloat16)
        expert_out = expert_out.reshape(1, local_experts, group * slot_cap, model_dim)
        back_rows = lax.all_to_all(expert_out, 'ep', 2, 0, tiled=True)
        back_rows = back_rows.reshape(num_experts * slot_cap, model_dim)
        picked = jnp.take(back_rows, slot_ids, axis=0).reshape(tok_n, top_n, model_dim)
        mixed = jnp.sum(gates_loc[:, :, None] * picked.astype(jnp.float32), axis=1)
        return mixed.astype(jnp.bfloat16)

    return jax.shard_map(local_layer, mesh=mesh, in_specs=(token_spec, token_spec, token_spec, expert_spec, expert_spec), out_specs=token_spec, check_vma=False)
```

profile of v0, /device:TPU:0, one launch (start us, length us, event | category | flops | bytes accessed | tf_op | source)
XLA Modules:
  0.0 153.9 jit_solution(9689288086985195338)
XLA Ops:
  0.0 0.8 copy.33
  0.9 0.1 eq.39
  1.0 0.1 reshape.114
  1.1 0.6 reduce-window.6
  1.7 0.2 slice_reduce_fusion
  2.1 0.1 reduce_sum.23
  2.3 0.7 compare_and_fusion
  3.1 0.8 convolution_convert_fusion
  4.0 34.6 %all_to_all.8 = bf16[8,1,64,2304]{3,2,1,0:T(8,128)(2,1)S(1)} all-to-all(bf16[8,1,64,2304]{3,2,1,0:T(8,128)(2,1)S(1)} %bitcast.62), channel_id=1, replica_groups=mesh['dp'=2,'ep'=8] {'ep'}, dimensions={0} | all-to-all | bytes 4718592 | tf_op jit(solution)/shard_map/all_to_all | solution.py:30
  38.6 20.4 %fusion.47 = bf16[512,5760]{1,0:T(8,128)(2,1)S(1)} fusion(bf16[1,2304,5760]{2,1,0:T(8,128)(2,1)} %param.8, bf16[512,2304]{1,0:T(8,128)(2,1)S(1)} %bitcast.63), kind=kOutput, calls=%bitcast_fusion.2.clone.1 | convolution fusion | flops 13616087040 | bytes 34799616 | tf_op jit(solution)/shard_map/ecm,emf->ecf/dot_general | solution.py:32
  59.0 18.1 %fusion.17 = bf16[1,1,512,2304]{3,2,1,0:T(8,128)(2,1)S(1)} fusion(bf16[1,5760,2304]{2,1,0:T(8,128)(2,1)} %param.9, bf16[512,5760]{1,0:T(8,128)(2,1)S(1)} %fusion.47), kind=kOutput, calls=%fused_computation.16 | convolution fusion | flops 13590724608 | bytes 34799616 | tf_op jit(solution)/shard_map/ecf,efm->ecm/dot_general | solution.py:34
  77.1 5.8 %copy.44 = bf16[1,1,512,2304]{3,1,0,2:T(2,128)(2,1)} copy(bf16[1,1,512,2304]{3,2,1,0:T(8,128)(2,1)S(1)} %fusion.17) | data formatting | bytes 4718592 | tf_op jit(solution)/shard_map/reshape | solution.py:35
  82.8 0.5 broadcast.74
  83.3 15.1 %reduce.2 = bf16[512,2304]{1,0:T(8,128)(2,1)S(1)} reduce(bf16[512,1,1,2304]{3,2,1,0:T(2,128)(2,1)} %bitcast.60, bf16[]{:T(256)} %broadcast.74), dimensions={1,2}, to_apply=%bitcast.58.reduce_sub_computation | reduce | bytes 4718594
  98.5 3.3 %reshape.131 = bf16[8,2,73728]{2,1,0:T(2,128)(2,1)} reshape(bf16[512,2304]{1,0:T(8,128)(2,1)S(1)} %reduce.2) | data formatting | bytes 4718592
  101.8 3.6 %all-to-all-start.1 = ((bf16[8,2,73728]{2,1,0:T(2,128)(2,1)}), bf16[8,2,73728]{2,1,0:T(2,128)(2,1)S(1)}, u32[]{:S(2)}, u32[]{:S(2)}) async-start(bf16[8,2,73728]{2,1,0:T(2,128)(2,1)} %reshape.131), calls=%async_computation.1 | async-start | bytes 4718592 | tf_op jit(solution)/shard_map/all_to_all | solution.py:36
  105.5 0.1 mul.68
  105.7 0.1 copy.36
  106.0 28.8 %all-to-all-done.1 = bf16[8,2,73728]{2,1,0:T(2,128)(2,1)S(1)} async-done(((bf16[8,2,73728]{2,1,0:T(2,128)(2,1)}), bf16[8,2,73728]{2,1,0:T(2,128)(2,1)S(1)}, u32[]{:S(2)}, u32[]{:S(2)}) %all-to-all-start.1) | async-done | bytes 2359328 | tf_op jit(solution)/shard_map/all_to_all | solution.py:36
  134.8 4.6 %reshape.132 = bf16[512,1,1,2304]{3,2,1,0:T(2,128)(2,1)} reshape(bf16[8,2,73728]{2,1,0:T(2,128)(2,1)S(1)} %all-to-all-done.1) | data formatting | bytes 4718592
  139.3 2.7 %copy.43 = bf16[1,1,512,2304]{3,2,0,1:T(8,128)(2,1)S(1)} copy(bf16[1,1,512,2304]{3,1,0,2:T(2,128)(2,1)} %bitcast.61) | data formatting | bytes 4718592
  142.0 2.4 %gather_fusion = bf16[256,2304]{1,0:T(8,128)(2,1)} fusion(bf16[512,2304]{1,0:T(8,128)(2,1)S(1)} %bitcast.59, s32[1024]{0:T(1024)S(1)} %pad_clamp_fusion), kind=kCustom, calls=%fused_computation | custom fusion | bytes 2360320 | tf_op jit(solution)/shard_map/jit(_take)/gather | solution.py:38
  144.4 2.8 %gather.7 = bf16[128,2,2304]{2,1,0:T(2,128)(2,1)S(1)} reshape(bf16[256,2304]{1,0:T(8,128)(2,1)} %gather_fusion) | data formatting | bytes 2359296 | tf_op jit(solution)/shard_map/jit(_take)/gather | solution.py:38
  147.3 6.7 %multiply_reduce_fusion = bf16[128,2304]{1,0:T(8,128)(2,1)} fusion(bf16[128,2,2304]{2,1,0:T(2,128)(2,1)S(1)} %gather.7, pred[128,2]{1,0:T(8,128)(4,1)S(1)} %copy.36, f32[128,2]{1,0:T(8,128)S(1)} %copy.32), kind=kLoop, calls=%fused_computation.18 | loop fusion | flops 2064384 | bytes 1770752 | tf_op jit(solution)/shard_map/reduce_sum | solution.py:39
  (19 shorter events, 0.6 us)
Async XLA Ops:
  0.0 3.1 %copy-start = (bf16[128,2304]{1,0:T(8,128)(2,1)S(1)}, bf16[128,2304]{1,0:T(8,128)(2,1)}, u32[]{:S(2)}) copy-start(bf16[128,2304]{1,0:T(8,128)(2,1)} %param.5) | copy-start | bytes 1769476
  98.4 7.0 %copy-start.2 = (s32[128,2]{0,1:T(2,128)S(1)}, s32[128,2]{0,1:T(2,128)}, u32[]{:S(2)}) copy-start(s32[128,2]{0,1:T(2,128)} %param.6) | copy-start | bytes 3076
  98.5 7.4 %copy-start.3 = (f32[128,2]{0,1:T(2,128)S(1)}, f32[128,2]{0,1:T(2,128)}, u32[]{:S(2)}) copy-start(f32[128,2]{0,1:T(2,128)} %param.7) | copy-start | bytes 3076
  101.8 33.0 %all-to-all-start.1 = ((bf16[8,2,73728]{2,1,0:T(2,128)(2,1)}), bf16[8,2,73728]{2,1,0:T(2,128)(2,1)S(1)}, u32[]{:S(2)}, u32[]{:S(2)}) async-start(bf16[8,2,73728]{2,1,0:T(2,128)(2,1)} %reshape.131), calls=%async_computation.1 | async-start | bytes 4718592 | tf_op jit(solution)/shard_map/all_to_all | solution.py:36
  142.0 12.0 %copy-start.1 = (bf16[128,2304]{1,0:T(8,128)(2,1)S(1)}, bf16[128,2304]{1,0:T(8,128)(2,1)}, u32[]{:S(2)}) copy-start(bf16[128,2304]{1,0:T(8,128)(2,1)} %param.5) | copy-start | bytes 1769476
where the time goes:
time: 154 us
  matrix products  39.3 us (26%)
  blocking collectives  34.6 us (22%)
  waiting for transfers between devices  28.8 us (19%)
  local copies, waits for them, and re-layouts  24.2 us (16%)
  other arithmetic  23.3 us (15%)
  starting transfers between devices  3.61 us (2%)
    all_to_all x1, blocking collectives, local_layer(): recv_rows = lax.all_to_all(send_rows, 'ep', 0, 2, tiled=True)  34.6 us
    all_to_all x1, waiting for transfers between devices, local_layer(): back_rows = lax.all_to_all(expert_out, 'ep', 2, 0, tiled=True)  28.8 us
    dot_general x1, matrix products, local_layer(): jnp.einsum('ecm,emf->ecf', recv_rows, w_up, preferred_element_type=jnp.fl...  20.4 us
    dot_general x1, matrix products, local_layer(): jnp.einsum('ecf,efm->ecm', hidden, w_down, preferred_element_type=jnp.flo...  18.1 us
    unnamed x1, other arithmetic  15.1 us
    unnamed x14, local copies, waits for them, and re-layouts  12.1 us
    reduce_sum x1, other arithmetic, local_layer(): mixed = jnp.sum(gates_loc[:, :, None] * picked.astype(jnp.float32), axis=1)  6.68 us
    reshape x1, local copies, waits for them, and re-layouts, local_layer(): expert_out.reshape(1, local_experts, group * slot_cap, model_dim)  5.76 us
  transfers between devices with their start and end apart: 1, of which 1 were waited for; matrix products, arithmetic and copies ran while one was open for 0% of the time, Pallas kernels for 0%

commit v1 on v0

v1 whole, which is shorter than its diff:
```python
import functools

import jax
import jax.numpy as jnp
from jax import lax
from jax.experimental import pallas as pl
from jax.experimental.pallas import tpu as pltpu
from jax.sharding import PartitionSpec as P

MESH = pl.DeviceIdType.MESH
TOK = 128
CAP = 64
EXP = 8
D = 2304
F = 5760
NU = 1024
U_FULL = F // NU
U_REM = F - U_FULL * NU
CW = 1152
NC = D // CW
OWN2_TILE = 2
RELAY_TILE = 4


def remote(src, dst, send_sem, recv_sem, dev):
    return pltpu.make_async_remote_copy(src_ref=src, dst_ref=dst, send_sem=send_sem, recv_sem=recv_sem, device_id={'ep': dev}, device_id_type=MESH)


def moe_kernel(x_hbm, ids_ref, gates_ref, wu_hbm, wd_hbm, y_hbm, wu, wd, xg, back, hid, xs, posg, post, sx, rx, sm, rm, sb, rb, sw, sl):
    me = lax.axis_index('ep')
    c = lax.rem(me, 2)
    x = lax.rem(me // 2, 2)
    y = me // 4

    def dev(yy, xx, cc):
        return yy * 4 + xx * 2 + cc

    partner = dev(y, x, 1 - c)
    first = dev(lax.rem(y + c, 2), lax.rem(x + 1 - c, 2), c)
    second = dev(lax.rem(y + 1 - c, 2), lax.rem(x + c, 2), c)
    others = [dev(lax.rem(y + dy, 2), lax.rem(x + dx, 2), lax.rem(c + dc, 2)) for dy, dx, dc in ((0, 0, 1), (0, 1, 0), (1, 0, 0), (0, 1, 1), (1, 0, 1), (1, 1, 0), (1, 1, 1))]

    def source(i, cc):
        lo, hi = lax.rem(i, 2), i // 2
        fx = lo * (1 - cc) + hi * cc
        fy = hi * (1 - cc) + lo * cc
        return dev(lax.rem(y + fy, 2), lax.rem(x + fx, 2), cc)

    own_load = pltpu.make_async_copy(x_hbm, xg.at[me], sl.at[0])
    own_load.start()

    def up_load(t):
        cols = pl.ds(pl.multiple_of(t * NU, 128), NU)
        return pltpu.make_async_copy(wu_hbm.at[0, :, cols], wu.at[:, cols], sw.at[t])

    def up_rem_load():
        cols = pl.ds(U_FULL * NU, U_REM)
        return pltpu.make_async_copy(wu_hbm.at[0, :, cols], wu.at[:, cols], sw.at[U_FULL])

    def down_load(n):
        cols = pl.ds(pl.multiple_of(n * CW, 128), CW)
        return pltpu.make_async_copy(wd_hbm.at[0, :, cols], wd.at[:, cols], sw.at[U_FULL + 1 + n])

    for t in range(U_FULL):
        up_load(t).start()
    up_rem_load().start()
    for n in range(NC):
        down_load(n).start()

    barrier = pltpu.get_barrier_semaphore()
    for other in others:
        pl.semaphore_signal(barrier, inc=1, device_id={'ep': other}, device_id_type=MESH)

    lane = lax.broadcasted_iota(jnp.int32, (TOK, TOK), 1)
    row = lax.broadcasted_iota(jnp.int32, (TOK, TOK), 0)
    id0 = ids_ref[:, 0:1]
    id1 = ids_ref[:, 1:2]
    hit = (id0 == lane) | (id1 == lane)
    lower = jnp.where(lane < row, 1.0, 0.0).astype(jnp.bfloat16)
    rank = jnp.dot(lower, jnp.where(hit, 1.0, 0.0).astype(jnp.bfloat16), preferred_element_type=jnp.float32)
    slot = jnp.where(hit, rank, -1.0)
    post[...] = slot
    posg[me] = slot.T[0:EXP]

    pl.semaphore_wait(barrier, EXP - 1)
    own_load.wait()

    own_first = remote(xg.at[me], xg.at[me], sx.at[0], rx.at[me], first)
    own_partner = remote(xg.at[me], xg.at[me], sx.at[1], rx.at[me], partner)
    own_second = remote(xg.at[me], xg.at[me], sx.at[2], rx.at[me], second)
    metas = [remote(posg.at[me], posg.at[me], sm.at[k], rm.at[me], other) for k, other in enumerate(others)]

    def arrived(s):
        return remote(xg.at[s], xg.at[s], sx.at[0], rx.at[s], partner)

    def meta_arrived(s):
        return remote(posg.at[s], posg.at[s], sm.at[0], rm.at[s], partner)

    def relay(i):
        s = source(i, c)
        return remote(xg.at[s], xg.at[s], sx.at[3 + i], rx.at[s], partner)

    def forward():
        s = source(1, c)
        return remote(xg.at[s], xg.at[s], sx.at[3], rx.at[s], second)

    for meta in metas:
        meta.start()
    own_first.start()
    own_partner.start()

    def up_tile(j, cols):
        z = jnp.dot(xs[...], wu[:, cols], preferred_element_type=jnp.float32)
        hid[jnp.minimum(j, 1), :, cols] = jax.nn.gelu(z, approximate=True).astype(jnp.bfloat16)

    def back_send(i, s, n):
        cols = pl.ds(pl.multiple_of(n * CW, 128), CW)
        return remote(xg.at[source(i, 1 - c), pl.ds(s * CAP, CAP), cols], back.at[me, :, cols], sb.at[(i * 2 + s) * NC + n], rb.at[me, n], source(i, s))

    def back_partner(n):
        cols = pl.ds(pl.multiple_of(n * CW, 128), CW)
        return remote(xg.at[partner, pl.ds(pl.multiple_of((1 - c) * CAP, CAP), CAP), cols], back.at[me, :, cols], sb.at[n], rb.at[me, n], partner)

    def phase(j, carry):
        @pl.when(j < 4)
        def _up():
            @pl.when(j == 0)
            def _():
                arrived(partner).wait_recv()
                meta_arrived(partner).wait_recv()

            @pl.when(j > 0)
            def _():
                arrived(source(j, 1 - c)).wait_recv()
                meta_arrived(source(j, 0)).wait_recv()
                meta_arrived(source(j, 1)).wait_recv()

            for s in range(2):
                s_id = source(j, s)
                where = posg[s_id, pl.ds(me, 1), :]
                slots = lax.broadcasted_iota(jnp.int32, (CAP, TOK), 0).astype(jnp.float32)
                pick = jnp.where(slots == where, 1.0, 0.0).astype(jnp.bfloat16)
                xs[s * CAP:(s + 1) * CAP, :] = jnp.dot(pick, xg[s_id], preferred_element_type=jnp.float32).astype(jnp.bfloat16)

            def tile(t, carry):
                @pl.when(j == 0)
                def _():
                    up_load(t).wait()

                    @pl.when(t == OWN2_TILE)
                    def _():
                        own_second.start()

                    @pl.when(t == RELAY_TILE)
                    def _():
                        arrived(source(1, c)).wait_recv()
                        relay(1).start()
                        forward().start()

                up_tile(j, pl.ds(pl.multiple_of(t * NU, 128), NU))
                return carry

            lax.fori_loop(0, U_FULL, tile, 0)

            @pl.when(j == 0)
            def _():
                up_rem_load().wait()

            up_tile(j, pl.ds(U_FULL * NU, U_REM))

        @pl.when((j == 1) | (j == 2))
        def _():
            arrived(source(j + 1, c)).wait_recv()
            relay(j + 1).start()

        @pl.when(j > 0)
        def _down():
            i = lax.rem(j, 4)

            def tile(n, carry):
                @pl.when(j == 1)
                def _():
                    down_load(n).wait()

                cols = pl.ds(pl.multiple_of(n * CW, 128), CW)
                o = jnp.dot(hid[jnp.minimum(i, 1)], wd[:, cols], preferred_element_type=jnp.float32).astype(jnp.bfloat16)
                xg[source(i, 1 - c), :, cols] = o

                @pl.when(i > 0)
                def _():
                    back_send(i, 0, n).start()
                    back_send(i, 1, n).start()

                @pl.when(i == 0)
                def _():
                    back_partner(n).start()
                    back[me, :, cols] = xg[partner, pl.ds(pl.multiple_of(c * CAP, CAP), CAP), cols]

                return carry

            lax.fori_loop(0, NC, tile, 0)

        return carry

    lax.fori_loop(0, 5, phase, 0)

    slot = post[...]
    parts = []
    for k in range(EXP // 2):
        low = lane < CAP
        at = jnp.where(low, slot[:, 2 * k:2 * k + 1], slot[:, 2 * k + 1:2 * k + 2])
        parts.append((at.astype(jnp.int32) == lane - jnp.where(low, 0, CAP), 2 * k + jnp.where(low, 0, 1)))
    picks = jnp.concatenate([jnp.concatenate([jnp.where(here & (expert == idj), 1.0, 0.0).astype(jnp.bfloat16) for here, expert in parts], axis=1) for idj in (id0, id1)], axis=0)
    g0 = gates_ref[:, 0:1]
    g1 = gates_ref[:, 1:2]

    def y_store(n):
        cols = pl.ds(n * CW, CW)
        return pltpu.make_async_copy(xs.at[:, cols], y_hbm.at[:, cols], sl.at[1 + n])

    for n in range(NC):
        cols = pl.ds(n * CW, CW)
        for other in others:
            remote(back.at[other, :, cols], back.at[other, :, cols], sb.at[0], rb.at[other, n], partner).wait_recv()
        rows = back[:, :, cols].reshape(EXP * CAP, CW)
        got = jnp.dot(picks, rows, preferred_element_type=jnp.float32)
        xs[:, cols] = (g0 * got[:TOK] + g1 * got[TOK:]).astype(jnp.bfloat16)
        y_store(n).start()

    own_first.wait_send()
    own_partner.wait_send()
    own_second.wait_send()
    forward().wait_send()
    for i in range(1, 4):
        relay(i).wait_send()
    for meta in metas:
        meta.wait_send()
    for n in range(NC):
        back_partner(n).wait_send()
        for i in (1, 2, 3):
            for s in range(2):
                back_send(i, s, n).wait_send()
    for n in range(NC):
        y_store(n).wait()


def solution(mesh):
    token_spec = P(('dp', 'ep'), None)
    expert_spec = P('ep', None, None)
    vmem = pl.BlockSpec(memory_space=pltpu.VMEM)
    anyspace = pl.BlockSpec(memory_space=pl.ANY)
    bf16, f32 = jnp.bfloat16, jnp.float32

    def local_layer(x_loc, ids_loc, gates_loc, w_up, w_down):
        return pl.pallas_call(
            moe_kernel,
            out_shape=jax.ShapeDtypeStruct((TOK, D), bf16),
            in_specs=[anyspace, vmem, vmem, anyspace, anyspace],
            out_specs=anyspace,
            scratch_shapes=[
                pltpu.VMEM((D, F), bf16),
                pltpu.VMEM((F, D), bf16),
                pltpu.VMEM((EXP, TOK, D), bf16),
                pltpu.VMEM((EXP, CAP, D), bf16),
                pltpu.VMEM((2, TOK, F), bf16),
                pltpu.VMEM((TOK, D), bf16),
                pltpu.VMEM((EXP, EXP, TOK), f32),
                pltpu.VMEM((TOK, TOK), f32),
                pltpu.SemaphoreType.DMA((7,)),
                pltpu.SemaphoreType.DMA((EXP,)),
                pltpu.SemaphoreType.DMA((7,)),
                pltpu.SemaphoreType.DMA((EXP,)),
                pltpu.SemaphoreType.DMA((8 * NC,)),
                pltpu.SemaphoreType.DMA((EXP, NC)),
                pltpu.SemaphoreType.DMA((U_FULL + 1 + NC,)),
                pltpu.SemaphoreType.DMA((1 + NC,)),
            ],
            compiler_params=pltpu.CompilerParams(vmem_limit_bytes=67043328, collective_id=0, has_side_effects=True),
        )(x_loc, ids_loc, gates_loc, w_up, w_down)

    return jax.shard_map(local_layer, mesh=mesh, in_specs=(token_spec, token_spec, token_spec, expert_spec, expert_spec), out_specs=token_spec, check_vma=False)
```

time: 154 us -> 81.9 us (0.53)
  the two profiles are of different devices: /device:TPU:0 before, /device:TPU:1 now
where the time goes in v1:
time: 81.9 us; the launch traced here: 81.7 us
  Pallas kernels  76.9 us (94%)
  local copies, waits for them, and re-layouts  4.73 us (6%)
    pallas_call x1, Pallas kernels, local_layer(): pl.pallas_call(moe_kernel, out_shape=jax.ShapeDtypeStruct((TOK, D), bf16)...  76.9 us
    unnamed x3, local copies, waits for them, and re-layouts  4.73 us

profile of v1, /device:TPU:1, one launch (start us, length us, event | category | flops | bytes accessed | tf_op | source)
XLA Modules:
  0.0 81.7 jit_solution(12392241357327081915)
XLA Ops:
  0.0 1.4 %copy.6.ids_ref = s32[128,2]{1,0:T(8,128)} copy(s32[128,2]{0,1:T(2,128)} %param.6) | data formatting | bytes 2048 | tf_op args[1]
  1.4 1.4 %copy.7.gates_ref = f32[128,2]{1,0:T(8,128)} copy(f32[128,2]{0,1:T(2,128)} %param.7) | data formatting | bytes 2048 | tf_op args[2]
  2.8 76.9 %shard_map.55 = bf16[128,2304]{1,0:T(8,128)(2,1)} custom-call(bf16[128,2304]{1,0:T(8,128)(2,1)} %x_hbm.1, s32[128,2]{1,0:T(8,128)} %copy.6.ids_ref, f32[128,2]{1,0:T(8,128)} %copy.7.gates_ref, bf16[1,2304,5760]{2,1,0:T(8,128)(2,1)} %wu_hbm.1, bf16[1,5760,2304]{2,1,0:T(8,128)(2,1)} %wd_hbm.1), custom_call_target="tpu_custom_call" | custom-call | tf_op jit(solution)/shard_map/pallas_call | solution.py:255
  79.7 1.9 %copy.9 = bf16[128,2304]{1,0:T(8,128)(2,1)} copy(bf16[128,2304]{1,0:T(8,128)(2,1)} %shard_map.55) | data formatting | bytes 1179648

commit v2 on v0

v2 whole, which is shorter than its diff:
```python
import functools

import jax
import jax.numpy as jnp
from jax import lax
from jax.experimental import pallas as pl
from jax.experimental.pallas import tpu as pltpu
from jax.sharding import PartitionSpec as P

MESH = pl.DeviceIdType.MESH
TOK = 128
CAP = 64
EXP = 8
D = 2304
F = 5760
NU = 1024
NT = -(-F // NU)
AHEAD = 4
DOWN = ((0, 1024), (1024, 1280))
MSG = ((0, 512), (512, 512), (1024, 768), (1792, 512))
NM = len(MSG)
SPLIT = 48
VMEM_LIMIT = 67043328


def remote(src, dst, send_sem, recv_sem, dev):
    return pltpu.make_async_remote_copy(src_ref=src, dst_ref=dst, send_sem=send_sem, recv_sem=recv_sem, device_id={'ep': dev}, device_id_type=MESH)


def moe_kernel(x_hbm, ids_ref, gates_ref, wu_hbm, wd_hbm, y_ref, wu, wd, xg, back, hid, xs, posg, post, sx, rx, sm, rm, sb, rb, rz, sw, sl):
    me = lax.axis_index('ep')
    c = lax.rem(me, 2)
    x = lax.rem(me // 2, 2)
    y = me // 4

    def dev(yy, xx, cc):
        return yy * 4 + xx * 2 + cc

    partner = dev(y, x, 1 - c)
    first = dev(lax.rem(y + c, 2), lax.rem(x + 1 - c, 2), c)
    second = dev(lax.rem(y + 1 - c, 2), lax.rem(x + c, 2), c)
    others = [dev(lax.rem(y + dy, 2), lax.rem(x + dx, 2), lax.rem(c + dc, 2)) for dy, dx, dc in ((0, 0, 1), (0, 1, 0), (1, 0, 0), (0, 1, 1), (1, 0, 1), (1, 1, 0), (1, 1, 1))]

    def source(i, cc):
        lo, hi = lax.rem(i, 2), i // 2
        fx = lo * (1 - cc) + hi * cc
        fy = hi * (1 - cc) + lo * cc
        return dev(lax.rem(y + fy, 2), lax.rem(x + fx, 2), cc)

    own_load = pltpu.make_async_copy(x_hbm, xg.at[me], sl.at[0])
    own_load.start()

    def up_cols(t):
        return pl.ds(t * NU, min(NU, F - t * NU))

    def down_cols(n):
        return pl.ds(*DOWN[n])

    def msg_cols(m):
        return pl.ds(*MSG[m])

    def up_load(t):
        return pltpu.make_async_copy(wu_hbm.at[0, :, up_cols(t)], wu.at[:, up_cols(t)], sw.at[t])

    def down_load(n):
        return pltpu.make_async_copy(wd_hbm.at[0, :, down_cols(n)], wd.at[:, down_cols(n)], sw.at[NT + n])

    barrier = pltpu.get_barrier_semaphore()
    for other in others:
        pl.semaphore_signal(barrier, inc=1, device_id={'ep': other}, device_id_type=MESH)

    lane = lax.broadcasted_iota(jnp.int32, (TOK, TOK), 1)
    row = lax.broadcasted_iota(jnp.int32, (TOK, TOK), 0)
    expert_row = lax.broadcasted_iota(jnp.int32, (EXP, TOK), 0)
    hit = (ids_ref[0:1, :] == expert_row) | (ids_ref[1:2, :] == expert_row)
    upper = jnp.where(row < lane, 1.0, 0.0).astype(jnp.bfloat16)
    rank = jnp.dot(jnp.where(hit, 1.0, 0.0).astype(jnp.bfloat16), upper, preferred_element_type=jnp.float32)
    slots = jnp.where(hit, rank, -1.0)
    posg[me] = slots
    pad = jnp.zeros((TOK - EXP - 4, TOK), jnp.float32)
    post[...] = jnp.concatenate([slots, ids_ref[...].astype(jnp.float32), gates_ref[...], pad], axis=0).T

    with jax.named_scope('own_load'):
        own_load.wait()
    for t in range(AHEAD):
        up_load(t).start()
    with jax.named_scope('barrier'):
        pl.semaphore_wait(barrier, EXP - 1)

    own_first = remote(xg.at[me], xg.at[me], sx.at[0], rx.at[me], first)
    own_partner = remote(xg.at[me], xg.at[me], sx.at[1], rx.at[me], partner)
    own_second = [remote(xg.at[me, rows], xg.at[me, rows], sx.at[2 + 5 * p], (rx.at[me], rz)[p], second) for p, rows in enumerate((pl.ds(0, SPLIT), pl.ds(SPLIT, TOK - SPLIT)))]
    metas = [remote(posg.at[me], posg.at[me], sm.at[k], rm.at[me], other) for k, other in enumerate(others)]

    def arrived(s):
        return remote(xg.at[s], xg.at[s], sx.at[0], rx.at[s], partner)

    def meta_arrived(s):
        return remote(posg.at[s], posg.at[s], sm.at[0], rm.at[s], partner)

    def relay(i):
        s = source(i, c)
        return remote(xg.at[s], xg.at[s], sx.at[3 + i], rx.at[s], partner)

    def forward():
        s = source(1, c)
        return remote(xg.at[s], xg.at[s], sx.at[3], rx.at[s], second)

    def back_send(i, s, m):
        return remote(xg.at[source(i, 1 - c), pl.ds(s * CAP, CAP), msg_cols(m)], back.at[me, :, msg_cols(m)], sb.at[(i * 2 + s) * NM + m], rb.at[me, m], source(i, s))

    def back_partner(m):
        return remote(xg.at[partner, pl.ds(pl.multiple_of((1 - c) * CAP, CAP), CAP), msg_cols(m)], back.at[me, :, msg_cols(m)], sb.at[m], rb.at[me, m], partner)

    def gather(i):
        for s in range(2):
            s_id = source(i, s)
            where = posg[s_id, pl.ds(me, 1), :]
            rank_row = lax.broadcasted_iota(jnp.int32, (CAP, TOK), 0).astype(jnp.float32)
            pick = jnp.where(rank_row == where, 1.0, 0.0).astype(jnp.bfloat16)
            xs[s * CAP:(s + 1) * CAP, :] = jnp.dot(pick, xg[s_id], preferred_element_type=jnp.float32).astype(jnp.bfloat16)

    def up_tile(h, t):
        z = jnp.dot(xs[...], wu[:, up_cols(t)], preferred_element_type=jnp.float32)
        hid[h, :, up_cols(t)] = jax.nn.gelu(z, approximate=True).astype(jnp.bfloat16)

    def down_tile(h, i, n):
        xg[source(i, 1 - c), :, down_cols(n)] = jnp.dot(hid[h], wd[:, down_cols(n)], preferred_element_type=jnp.float32).astype(jnp.bfloat16)

    def own_down(n):
        down_tile(0, 0, n)
        for m in (2 * n, 2 * n + 1):
            back_partner(m).start()
        back[me, :, down_cols(n)] = xg[partner, pl.ds(pl.multiple_of(c * CAP, CAP), CAP), down_cols(n)]

    with jax.named_scope('start'):
        for meta in metas:
            meta.start()
        own_first.start()
        own_partner.start()
        for t in range(AHEAD, NT):
            up_load(t).start()
    with jax.named_scope('wait_partner'):
        arrived(partner).wait_recv()
        meta_arrived(partner).wait_recv()
    with jax.named_scope('up0'):
        gather(0)
        for t in range(NT):
            up_load(t).wait()
            if t == AHEAD - 1:
                down_load(0).start()
            if t == NT - 1:
                own_second[0].start()
                down_load(1).start()
            up_tile(0, t)
    with jax.named_scope('wait_f'):
        arrived(source(1, c)).wait_recv()
        relay(1).start()
        forward().start()
        own_second[1].start()
    with jax.named_scope('own_down'):
        down_load(0).wait()
        own_down(0)

    def chunk(k, carry):
        i = jnp.where(k == 1, 1, 5 - k)
        with jax.named_scope('wait_chunk'):
            arrived(source(i, 1 - c)).wait_recv()
            meta_arrived(source(i, 0)).wait_recv()
            meta_arrived(source(i, 1)).wait_recv()
        with jax.named_scope('up'):
            gather(i)
            for t in range(NT):
                up_tile(1, t)

        for n in range(2):
            with jax.named_scope('down'):
                down_tile(1, i, n)
                for m in (2 * n, 2 * n + 1):
                    for s in range(2):
                        back_send(i, s, m).start()
            if n == 0:
                with jax.named_scope('wait_direct'):
                    @pl.when(k == 1)
                    def _():
                        down_load(1).wait()

                    @pl.when(k == 2)
                    def _():
                        remote(xg.at[source(2, c), pl.ds(SPLIT, TOK - SPLIT)], xg.at[source(2, c), pl.ds(SPLIT, TOK - SPLIT)], sx.at[0], rz, partner).wait_recv()
                        remote(xg.at[source(2, c), pl.ds(0, SPLIT)], xg.at[source(2, c), pl.ds(0, SPLIT)], sx.at[0], rx.at[source(2, c)], partner).wait_recv()
                        relay(2).start()

                    @pl.when(k == 1)
                    def _():
                        arrived(source(3, c)).wait_recv()
                        relay(3).start()
        return carry

    lax.fori_loop(1, 4, chunk, 0)
    with jax.named_scope('own_down'):
        own_down(1)

    cols8 = post[...]
    low = lane < CAP
    parts = []
    for k in range(EXP // 2):
        at = jnp.where(low, cols8[:, 2 * k:2 * k + 1], cols8[:, 2 * k + 1:2 * k + 2])
        here = at == (lane - jnp.where(low, 0, CAP)).astype(jnp.float32)
        parts.append((here, (2 * k + jnp.where(low, 0, 1)).astype(jnp.float32)))
    choice = [cols8[:, EXP + j:EXP + j + 1] for j in range(2)]
    picks = jnp.concatenate([jnp.concatenate([jnp.where(here & (expert == idj), 1.0, 0.0).astype(jnp.bfloat16) for here, expert in parts], axis=1) for idj in choice], axis=0)
    g0 = cols8[:, EXP + 2:EXP + 3]
    g1 = cols8[:, EXP + 3:EXP + 4]

    for m in range(NM):
        cols = msg_cols(m)
        with jax.named_scope('wait_back'):
            for other in others:
                remote(back.at[other, :, cols], back.at[other, :, cols], sb.at[0], rb.at[other, m], partner).wait_recv()
        with jax.named_scope('combine'):
            rows = back[:, :, cols].reshape(EXP * CAP, MSG[m][1])
            got = jnp.dot(picks, rows, preferred_element_type=jnp.float32)
            y_ref[:, cols] = (g0 * got[:TOK] + g1 * got[TOK:]).astype(jnp.bfloat16)

    own_first.wait_send()
    own_partner.wait_send()
    for piece in own_second:
        piece.wait_send()
    forward().wait_send()
    for i in range(1, 4):
        relay(i).wait_send()
    for meta in metas:
        meta.wait_send()
    for m in range(NM):
        back_partner(m).wait_send()
        for i in range(1, 4):
            for s in range(2):
                back_send(i, s, m).wait_send()


def solution(mesh):
    token_spec = P(('dp', 'ep'), None)
    expert_spec = P('ep', None, None)
    vmem = pl.BlockSpec(memory_space=pltpu.VMEM)
    anyspace = pl.BlockSpec(memory_space=pl.ANY)
    bf16, f32 = jnp.bfloat16, jnp.float32

    def local_layer(x_loc, ids_loc, gates_loc, w_up, w_down):
        return pl.pallas_call(
            moe_kernel,
            out_shape=jax.ShapeDtypeStruct((TOK, D), bf16),
            in_specs=[anyspace, vmem, vmem, anyspace, anyspace],
            out_specs=vmem,
            scratch_shapes=[
                pltpu.VMEM((D, F), bf16),
                pltpu.VMEM((F, D), bf16),
                pltpu.VMEM((EXP, TOK, D), bf16),
                pltpu.VMEM((EXP, CAP, D), bf16),
                pltpu.VMEM((2, TOK, F), bf16),
                pltpu.VMEM((TOK, D), bf16),
                pltpu.VMEM((EXP, EXP, TOK), f32),
                pltpu.VMEM((TOK, TOK), f32),
                pltpu.SemaphoreType.DMA((8,)),
                pltpu.SemaphoreType.DMA((EXP,)),
                pltpu.SemaphoreType.DMA((7,)),
                pltpu.SemaphoreType.DMA((EXP,)),
                pltpu.SemaphoreType.DMA((8 * NM,)),
                pltpu.SemaphoreType.DMA((EXP, NM)),
                pltpu.SemaphoreType.DMA,
                pltpu.SemaphoreType.DMA((NT + 2,)),
                pltpu.SemaphoreType.DMA((1,)),
            ],
            compiler_params=pltpu.CompilerParams(vmem_limit_bytes=VMEM_LIMIT, collective_id=0, has_side_effects=True),
        )(x_loc, ids_loc.T, gates_loc.T, w_up, w_down)

    return jax.shard_map(local_layer, mesh=mesh, in_specs=(token_spec, token_spec, token_spec, expert_spec, expert_spec), out_specs=token_spec, check_vma=False)
```

time: 154 us -> 58.5 us (0.38)
  Pallas kernels: 0 us -> 56.3 us
  matrix products: 39.3 us -> 0 us
  blocking collectives: 34.6 us -> 0 us
  waiting for transfers between devices: 28.8 us -> 0 us
  other arithmetic: 23.3 us -> 0 us
  local copies, waits for them, and re-layouts: 24.2 us -> 1.92 us
  starting transfers between devices: 3.61 us -> 0 us
    pallas_call x0 -> x1, Pallas kernels: none -> 56.3 us  [local_layer(): pl.pallas_call(moe_kernel, out_shape=jax.ShapeDtypeStruct((TOK, D), bf16)...]
    dot_general x3 -> x0, matrix products: 39.3 us -> none  [the longest x1 20.4 us: local_layer(): jnp.einsum('ecm,emf->ecf', recv_rows, w_up, preferred_element_type=jnp.fl...]
    all_to_all x1 -> x0, blocking collectives: 34.6 us -> none  [local_layer(): recv_rows = lax.all_to_all(send_rows, 'ep', 0, 2, tiled=True)]
    all_to_all x1 -> x0, waiting for transfers between devices: 28.8 us -> none  [local_layer(): back_rows = lax.all_to_all(expert_out, 'ep', 2, 0, tiled=True)]
    unnamed x1 -> x0, other arithmetic: 15.1 us -> none
    unnamed x14 -> x1, local copies, waits for them, and re-layouts: 12.1 us -> 1.92 us
    reduce_sum x2 -> x0, other arithmetic: 6.77 us -> none  [the longest x1 6.68 us: local_layer(): mixed = jnp.sum(gates_loc[:, :, None] * picked.astype(jnp.float32), axis=1)]
    reshape x2 -> x0, local copies, waits for them, and re-layouts: 5.9 us -> none  [the longest x1 5.76 us: local_layer(): expert_out.reshape(1, local_experts, group * slot_cap, model_dim)]
  transfers between devices with their start and end apart: 1 -> 0, of which waited for: 1 -> 0; matrix products, arithmetic and copies ran while one was open for 0% -> 0% of each run, Pallas kernels for 0% -> 0%
where the time goes in v2:
time: 58.5 us; the launch traced here: 58.3 us
  Pallas kernels  56.3 us (96%)
  local copies, waits for them, and re-layouts  1.92 us (3%)
    pallas_call x1, Pallas kernels, local_layer(): pl.pallas_call(moe_kernel, out_shape=jax.ShapeDtypeStruct((TOK, D), bf16)...  56.3 us
    unnamed x1, local copies, waits for them, and re-layouts  1.92 us

profile of v2, /device:TPU:0, one launch (start us, length us, event | category | flops | bytes accessed | tf_op | source)
XLA Modules:
  0.0 58.3 jit_solution(17876557840790698781)
XLA Ops:
  0.0 56.3 %shard_map.55 = bf16[128,2304]{1,0:T(8,128)(2,1)} custom-call(bf16[128,2304]{1,0:T(8,128)(2,1)} %x_hbm.1, s32[2,128]{1,0:T(2,128)} %bitcast.2, f32[2,128]{1,0:T(2,128)} %bitcast.3, bf16[1,2304,5760]{2,1,0:T(8,128)(2,1)} %wu_hbm.1, bf16[1,5760,2304]{2,1,0:T(8,128)(2,1)} %wd_hbm.1), custom_call_target="tpu_custom_call" | custom-call | tf_op jit(solution)/shard_map/pallas_call | solution.py:250
  56.4 1.9 %copy.7 = bf16[128,2304]{1,0:T(8,128)(2,1)} copy(bf16[128,2304]{1,0:T(8,128)(2,1)} %shard_map.55) | data formatting | bytes 1179648

commit v3 on v2

--- a/solution.py
+++ b/solution.py
@@ -15,11 +15,12 @@
 F = 5760
 NU = 1024
 NT = -(-F // NU)
-AHEAD = 4
+F_TILE = 4
+AHEAD = 2
 DOWN = ((0, 1024), (1024, 1280))
 MSG = ((0, 512), (512, 512), (1024, 768), (1792, 512))
 NM = len(MSG)
-SPLIT = 48
+HALF = TOK // 2
 VMEM_LIMIT = 67043328
 
 
@@ -27,7 +28,7 @@
     return pltpu.make_async_remote_copy(src_ref=src, dst_ref=dst, send_sem=send_sem, recv_sem=recv_sem, device_id={'ep': dev}, device_id_type=MESH)
 
 
-def moe_kernel(x_hbm, ids_ref, gates_ref, wu_hbm, wd_hbm, y_ref, wu, wd, xg, back, hid, xs, posg, post, sx, rx, sm, rm, sb, rb, rz, sw, sl):
+def moe_kernel(x_hbm, ids_hbm, gates_hbm, wu_hbm, wd_hbm, y_ref, ids_ref, gates_ref, wu, wd, xg, back, hid, xs, posg, post, sx, rx, sm, rm, sb, rb, sw, sl):
     me = lax.axis_index('ep')
     c = lax.rem(me, 2)
     x = lax.rem(me // 2, 2)
@@ -47,6 +48,13 @@
         fy = hi * (1 - cc) + lo * cc
         return dev(lax.rem(y + fy, 2), lax.rem(x + fx, 2), cc)
 
+    barrier = pltpu.get_barrier_semaphore()
+    for other in (partner, first, second):
+        pl.semaphore_signal(barrier, inc=1, device_id={'ep': other}, device_id_type=MESH)
+    ids_load = pltpu.make_async_copy(ids_hbm, ids_ref, sl.at[1])
+    gates_load = pltpu.make_async_copy(gates_hbm, gates_ref, sl.at[2])
+    ids_load.start()
+    gates_load.start()
     own_load = pltpu.make_async_copy(x_hbm, xg.at[me], sl.at[0])
     own_load.start()
 
@@ -65,10 +73,8 @@
     def down_load(n):
         return pltpu.make_async_copy(wd_hbm.at[0, :, down_cols(n)], wd.at[:, down_cols(n)], sw.at[NT + n])
 
-    barrier = pltpu.get_barrier_semaphore()
-    for other in others:
-        pl.semaphore_signal(barrier, inc=1, device_id={'ep': other}, device_id_type=MESH)
-
+    ids_load.wait()
+    gates_load.wait()
     lane = lax.broadcasted_iota(jnp.int32, (TOK, TOK), 1)
     row = lax.broadcasted_iota(jnp.int32, (TOK, TOK), 0)
     expert_row = lax.broadcasted_iota(jnp.int32, (EXP, TOK), 0)
@@ -85,26 +91,37 @@
     for t in range(AHEAD):
         up_load(t).start()
     with jax.named_scope('barrier'):
-        pl.semaphore_wait(barrier, EXP - 1)
-
-    own_first = remote(xg.at[me], xg.at[me], sx.at[0], rx.at[me], first)
-    own_partner = remote(xg.at[me], xg.at[me], sx.at[1], rx.at[me], partner)
-    own_second = [remote(xg.at[me, rows], xg.at[me, rows], sx.at[2 + 5 * p], (rx.at[me], rz)[p], second) for p, rows in enumerate((pl.ds(0, SPLIT), pl.ds(SPLIT, TOK - SPLIT)))]
-    metas = [remote(posg.at[me], posg.at[me], sm.at[k], rm.at[me], other) for k, other in enumerate(others)]
-
-    def arrived(s):
-        return remote(xg.at[s], xg.at[s], sx.at[0], rx.at[s], partner)
+        pl.semaphore_wait(barrier, 3)
+
+    def block(s, k, p, to):
+        rows = pl.ds(p * HALF, HALF)
+        return remote(xg.at[s, rows], xg.at[s, rows], sx.at[k, p], rx.at[s, p], to)
+
+    def own(k, p):
+        return block(me, k, p, (first, partner, second)[k])
+
+    def forward(p):
+        return block(source(1, c), 3, p, second)
+
+    def relay(i, p):
+        return block(source(i, c), 3 + i, p, partner)
+
+    def arrived(s, p):
+        block(s, 0, p, partner).wait_recv()
 
     def meta_arrived(s):
-        return remote(posg.at[s], posg.at[s], sm.at[0], rm.at[s], partner)
-
-    def relay(i):
-        s = source(i, c)
-        return remote(xg.at[s], xg.at[s], sx.at[3 + i], rx.at[s], partner)
-
-    def forward():
-        s = source(1, c)
-        return remote(xg.at[s], xg.at[s], sx.at[3], rx.at[s], second)
+        meta(s, 0, partner).wait_recv()
+
+    def meta(s, k, to):
+        return remote(posg.at[s], posg.at[s], sm.at[k], rm.at[s], to)
+
+    own_metas = [meta(me, k, to) for k, to in enumerate((first, partner, second))]
+
+    def forward_meta():
+        return meta(source(1, c), 3, second)
+
+    def relay_meta(i):
+        return meta(source(i, c), 3 + i, partner)
 
     def back_send(i, s, m):
         return remote(xg.at[source(i, 1 - c), pl.ds(s * CAP, CAP), msg_cols(m)], back.at[me, :, msg_cols(m)], sb.at[(i * 2 + s) * NM + m], rb.at[me, m], source(i, s))
@@ -134,44 +151,57 @@
         back[me, :, down_cols(n)] = xg[partner, pl.ds(pl.multiple_of(c * CAP, CAP), CAP), down_cols(n)]
 
     with jax.named_scope('start'):
-        for meta in metas:
-            meta.start()
-        own_first.start()
-        own_partner.start()
-        for t in range(AHEAD, NT):
+        for own_meta in own_metas:
+            own_meta.start()
+        for k in range(2):
+            for p in range(2):
+                own(k, p).start()
+        for t in range(AHEAD, 4):
             up_load(t).start()
     with jax.named_scope('wait_partner'):
-        arrived(partner).wait_recv()
-        meta_arrived(partner).wait_recv()
+        meta_arrived(partner)
+        for p in range(2):
+            arrived(partner, p)
     with jax.named_scope('up0'):
         gather(0)
         for t in range(NT):
             up_load(t).wait()
-            if t == AHEAD - 1:
+            if t < 2:
+                up_load(4 + t).start()
+            if t == 2:
                 down_load(0).start()
+            if t == F_TILE:
+                with jax.named_scope('wait_f0'):
+                    meta_arrived(source(1, c))
+                    arrived(source(1, c), 0)
+                forward_meta().start()
+                forward(0).start()
+                relay_meta(1).start()
+                relay(1, 0).start()
             if t == NT - 1:
-                own_second[0].start()
                 down_load(1).start()
             up_tile(0, t)
-    with jax.named_scope('wait_f'):
-        arrived(source(1, c)).wait_recv()
-        relay(1).start()
-        forward().start()
-        own_second[1].start()
-    with jax.named_scope('own_down'):
-        down_load(0).wait()
-        own_down(0)
+    with jax.named_scope('wait_f1'):
+        arrived(source(1, c), 1)
+        forward(1).start()
+        relay(1, 1).start()
+        for p in range(2):
+            own(2, p).start()
 
     def chunk(k, carry):
         i = jnp.where(k == 1, 1, 5 - k)
         with jax.named_scope('wait_chunk'):
-            arrived(source(i, 1 - c)).wait_recv()
-            meta_arrived(source(i, 0)).wait_recv()
-            meta_arrived(source(i, 1)).wait_recv()
+            meta_arrived(source(i, 1 - c))
+            for p in range(2):
+                arrived(source(i, 1 - c), p)
         with jax.named_scope('up'):
             gather(i)
             for t in range(NT):
                 up_tile(1, t)
+
+        @pl.when(k == 1)
+        def _():
+            down_load(0).wait()
 
         for n in range(2):
             with jax.named_scope('down'):
@@ -185,20 +215,19 @@
                     def _():
                         down_load(1).wait()
 
-                    @pl.when(k == 2)
+                    @pl.when(k < 3)
                     def _():
-                        remote(xg.at[source(2, c), pl.ds(SPLIT, TOK - SPLIT)], xg.at[source(2, c), pl.ds(SPLIT, TOK - SPLIT)], sx.at[0], rz, partner).wait_recv()
-                        remote(xg.at[source(2, c), pl.ds(0, SPLIT)], xg.at[source(2, c), pl.ds(0, SPLIT)], sx.at[0], rx.at[source(2, c)], partner).wait_recv()
-                        relay(2).start()
-
-                    @pl.when(k == 1)
-                    def _():
-                        arrived(source(3, c)).wait_recv()
-                        relay(3).start()
+                        after = 4 - k
+                        meta_arrived(source(after, c))
+                        relay_meta(after).start()
+                        for p in range(2):
+                            arrived(source(after, c), p)
+                            relay(after, p).start()
         return carry
 
     lax.fori_loop(1, 4, chunk, 0)
     with jax.named_scope('own_down'):
+        own_down(0)
         own_down(1)
 
     cols8 = post[...]
@@ -223,15 +252,17 @@
             got = jnp.dot(picks, rows, preferred_element_type=jnp.float32)
             y_ref[:, cols] = (g0 * got[:TOK] + g1 * got[TOK:]).astype(jnp.bfloat16)
 
-    own_first.wait_send()
-    own_partner.wait_send()
-    for piece in own_second:
-        piece.wait_send()
-    forward().wait_send()
+    for p in range(2):
+        for k in range(3):
+            own(k, p).wait_send()
+        forward(p).wait_send()
+        for i in range(1, 4):
+            relay(i, p).wait_send()
+    forward_meta().wait_send()
     for i in range(1, 4):
-        relay(i).wait_send()
-    for meta in metas:
-        meta.wait_send()
+        relay_meta(i).wait_send()
+    for own_meta in own_metas:
+        own_meta.wait_send()
     for m in range(NM):
         back_partner(m).wait_send()
         for i in range(1, 4):
@@ -250,9 +281,11 @@
         return pl.pallas_call(
             moe_kernel,
             out_shape=jax.ShapeDtypeStruct((TOK, D), bf16),
-            in_specs=[anyspace, vmem, vmem, anyspace, anyspace],
+            in_specs=[anyspace] * 5,
             out_specs=vmem,
             scratch_shapes=[
+                pltpu.VMEM((2, TOK), jnp.int32),
+                pltpu.VMEM((2, TOK), f32),
                 pltpu.VMEM((D, F), bf16),
                 pltpu.VMEM((F, D), bf16),
                 pltpu.VMEM((EXP, TOK, D), bf16),
@@ -261,15 +294,14 @@
                 pltpu.VMEM((TOK, D), bf16),
                 pltpu.VMEM((EXP, EXP, TOK), f32),
                 pltpu.VMEM((TOK, TOK), f32),
-                pltpu.SemaphoreType.DMA((8,)),
-                pltpu.SemaphoreType.DMA((EXP,)),
+                pltpu.SemaphoreType.DMA((7, 2)),
+                pltpu.SemaphoreType.DMA((EXP, 2)),
                 pltpu.SemaphoreType.DMA((7,)),
                 pltpu.SemaphoreType.DMA((EXP,)),
                 pltpu.SemaphoreType.DMA((8 * NM,)),
                 pltpu.SemaphoreType.DMA((EXP, NM)),
-                pltpu.SemaphoreType.DMA,
                 pltpu.SemaphoreType.DMA((NT + 2,)),
-                pltpu.SemaphoreType.DMA((1,)),
+                pltpu.SemaphoreType.DMA((3,)),
             ],
             compiler_params=pltpu.CompilerParams(vmem_limit_bytes=VMEM_LIMIT, collective_id=0, has_side_effects=True),
         )(x_loc, ids_loc.T, gates_loc.T, w_up, w_down)

time: 58.5 us -> 56.4 us (0.964)
  Pallas kernels: 56.3 us -> 54.3 us
    pallas_call x1, Pallas kernels: 56.3 us -> 54.3 us  [local_layer(): pl.pallas_call(moe_kernel, out_shape=jax.ShapeDtypeStruct((TOK, D), bf16)...]
where the time goes in v3:
time: 56.4 us; the launch traced here: 56.3 us
  Pallas kernels  54.3 us (96%)
  local copies, waits for them, and re-layouts  1.92 us (3%)
    pallas_call x1, Pallas kernels, local_layer(): pl.pallas_call(moe_kernel, out_shape=jax.ShapeDtypeStruct((TOK, D), bf16)...  54.3 us
    unnamed x1, local copies, waits for them, and re-layouts  1.92 us

profile of v3, /device:TPU:0, one launch (start us, length us, event | category | flops | bytes accessed | tf_op | source)
XLA Modules:
  0.0 56.3 jit_solution(1322056701645515702)
XLA Ops:
  0.0 54.3 %shard_map.55 = bf16[128,2304]{1,0:T(8,128)(2,1)} custom-call(bf16[128,2304]{1,0:T(8,128)(2,1)} %x_hbm.1, s32[2,128]{1,0:T(2,128)} %bitcast.2, f32[2,128]{1,0:T(2,128)} %bitcast.3, bf16[1,2304,5760]{2,1,0:T(8,128)(2,1)} %wu_hbm.1, bf16[1,5760,2304]{2,1,0:T(8,128)(2,1)} %wd_hbm.1), custom_call_target="tpu_custom_call" | custom-call | tf_op jit(solution)/shard_map/pallas_call | solution.py:281
  54.4 1.9 %copy.7 = bf16[128,2304]{1,0:T(8,128)(2,1)} copy(bf16[128,2304]{1,0:T(8,128)(2,1)} %shard_map.55) | data formatting | bytes 1179648

commit v4 on v3

--- a/solution.py
+++ b/solution.py
@@ -15,13 +15,14 @@
 F = 5760
 NU = 1024
 NT = -(-F // NU)
-F_TILE = 4
+F_TILE = 3
 AHEAD = 2
-DOWN = ((0, 1024), (1024, 1280))
-MSG = ((0, 512), (512, 512), (1024, 768), (1792, 512))
+DOWN = ((0, 512), (512, 1792))
+MSG = ((0, 512), (512, 640), (1152, 640), (1792, 512))
+BLOCK_MSGS = ((0,), (1, 2, 3))
 NM = len(MSG)
 HALF = TOK // 2
-VMEM_LIMIT = 67043328
+VMEM_LIMIT = 66400000
 
 
 def remote(src, dst, send_sem, recv_sem, dev):
@@ -73,6 +74,74 @@
     def down_load(n):
         return pltpu.make_async_copy(wd_hbm.at[0, :, down_cols(n)], wd.at[:, down_cols(n)], sw.at[NT + n])
 
+    with jax.named_scope('own_load'):
+        own_load.wait()
+    for t in range(AHEAD):
+        up_load(t).start()
+    with jax.named_scope('barrier'):
+        pl.semaphore_wait(barrier, 3)
+
+    def block(s, k, p, to):
+        rows = pl.ds(p * HALF, HALF)
+        return remote(xg.at[s, rows], xg.at[s, rows], sx.at[k, p], rx.at[s, p], to)
+
+    def own(k, p):
+        return block(me, k, p, (first, partner, second)[k])
+
+    def forward(p):
+        return block(source(1, c), 3, p, second)
+
+    def relay(i, p):
+        return block(source(i, c), 3 + i, p, partner)
+
+    def arrived(s, p):
+        block(s, 0, p, partner).wait_recv()
+
+    def meta_arrived(s):
+        meta(s, 0, partner).wait_recv()
+
+    def meta(s, k, to):
+        return remote(posg.at[s], posg.at[s], sm.at[k], rm.at[s], to)
+
+    own_metas = [meta(me, k, to) for k, to in enumerate((first, partner, second))]
+
+    def forward_meta():
+        return meta(source(1, c), 3, second)
+
+    def relay_meta(i):
+        return meta(source(i, c), 3 + i, partner)
+
+    def back_send(i, s, m):
+        return remote(xg.at[source(i, 1 - c), pl.ds(s * CAP, CAP), msg_cols(m)], back.at[me, :, msg_cols(m)], sb.at[(i * 2 + s) * NM + m], rb.at[me, m], source(i, s))
+
+    def back_partner(m):
+        return remote(xg.at[partner, pl.ds(pl.multiple_of((1 - c) * CAP, CAP), CAP), msg_cols(m)], back.at[me, :, msg_cols(m)], sb.at[m], rb.at[me, m], partner)
+
+    def gather(i):
+        for s in range(2):
+            s_id = source(i, s)
+            where = posg[s_id, pl.ds(me, 1), :]
+            rank_row = lax.broadcasted_iota(jnp.int32, (CAP, TOK), 0).astype(jnp.float32)
+            pick = jnp.where(rank_row == where, 1.0, 0.0).astype(jnp.bfloat16)
+            xs[s * CAP:(s + 1) * CAP, :] = jnp.dot(pick, xg[s_id], preferred_element_type=jnp.float32).astype(jnp.bfloat16)
+
+    def up_tile(h, t):
+        z = jnp.dot(xs[...], wu[:, up_cols(t)], preferred_element_type=jnp.float32)
+        hid[h, :, up_cols(t)] = jax.nn.gelu(z, approximate=True).astype(jnp.bfloat16)
+
+    def down_tile(h, i, n):
+        xg[source(i, 1 - c), :, down_cols(n)] = jnp.dot(hid[h], wd[:, down_cols(n)], preferred_element_type=jnp.float32).astype(jnp.bfloat16)
+
+    def own_down(n):
+        down_tile(0, 0, n)
+        for m in BLOCK_MSGS[n]:
+            back_partner(m).start()
+        back[me, :, down_cols(n)] = xg[partner, pl.ds(pl.multiple_of(c * CAP, CAP), CAP), down_cols(n)]
+
+    own(0, 0).start()
+    own(1, 0).start()
+    for t in range(AHEAD, 4):
+        up_load(t).start()
     ids_load.wait()
     gates_load.wait()
     lane = lax.broadcasted_iota(jnp.int32, (TOK, TOK), 1)
@@ -85,79 +154,10 @@
     posg[me] = slots
     pad = jnp.zeros((TOK - EXP - 4, TOK), jnp.float32)
     post[...] = jnp.concatenate([slots, ids_ref[...].astype(jnp.float32), gates_ref[...], pad], axis=0).T
-
-    with jax.named_scope('own_load'):
-        own_load.wait()
-    for t in range(AHEAD):
-        up_load(t).start()
-    with jax.named_scope('barrier'):
-        pl.semaphore_wait(barrier, 3)
-
-    def block(s, k, p, to):
-        rows = pl.ds(p * HALF, HALF)
-        return remote(xg.at[s, rows], xg.at[s, rows], sx.at[k, p], rx.at[s, p], to)
-
-    def own(k, p):
-        return block(me, k, p, (first, partner, second)[k])
-
-    def forward(p):
-        return block(source(1, c), 3, p, second)
-
-    def relay(i, p):
-        return block(source(i, c), 3 + i, p, partner)
-
-    def arrived(s, p):
-        block(s, 0, p, partner).wait_recv()
-
-    def meta_arrived(s):
-        meta(s, 0, partner).wait_recv()
-
-    def meta(s, k, to):
-        return remote(posg.at[s], posg.at[s], sm.at[k], rm.at[s], to)
-
-    own_metas = [meta(me, k, to) for k, to in enumerate((first, partner, second))]
-
-    def forward_meta():
-        return meta(source(1, c), 3, second)
-
-    def relay_meta(i):
-        return meta(source(i, c), 3 + i, partner)
-
-    def back_send(i, s, m):
-        return remote(xg.at[source(i, 1 - c), pl.ds(s * CAP, CAP), msg_cols(m)], back.at[me, :, msg_cols(m)], sb.at[(i * 2 + s) * NM + m], rb.at[me, m], source(i, s))
-
-    def back_partner(m):
-        return remote(xg.at[partner, pl.ds(pl.multiple_of((1 - c) * CAP, CAP), CAP), msg_cols(m)], back.at[me, :, msg_cols(m)], sb.at[m], rb.at[me, m], partner)
-
-    def gather(i):
-        for s in range(2):
-            s_id = source(i, s)
-            where = posg[s_id, pl.ds(me, 1), :]
-            rank_row = lax.broadcasted_iota(jnp.int32, (CAP, TOK), 0).astype(jnp.float32)
-            pick = jnp.where(rank_row == where, 1.0, 0.0).astype(jnp.bfloat16)
-            xs[s * CAP:(s + 1) * CAP, :] = jnp.dot(pick, xg[s_id], preferred_element_type=jnp.float32).astype(jnp.bfloat16)
-
-    def up_tile(h, t):
-        z = jnp.dot(xs[...], wu[:, up_cols(t)], preferred_element_type=jnp.float32)
-        hid[h, :, up_cols(t)] = jax.nn.gelu(z, approximate=True).astype(jnp.bfloat16)
-
-    def down_tile(h, i, n):
-        xg[source(i, 1 - c), :, down_cols(n)] = jnp.dot(hid[h], wd[:, down_cols(n)], preferred_element_type=jnp.float32).astype(jnp.bfloat16)
-
-    def own_down(n):
-        down_tile(0, 0, n)
-        for m in (2 * n, 2 * n + 1):
-            back_partner(m).start()
-        back[me, :, down_cols(n)] = xg[partner, pl.ds(pl.multiple_of(c * CAP, CAP), CAP), down_cols(n)]
-
-    with jax.named_scope('start'):
-        for own_meta in own_metas:
-            own_meta.start()
-        for k in range(2):
-            for p in range(2):
-                own(k, p).start()
-        for t in range(AHEAD, 4):
-            up_load(t).start()
+    for own_meta in own_metas:
+        own_meta.start()
+    own(0, 1).start()
+    own(1, 1).start()
     with jax.named_scope('wait_partner'):
         meta_arrived(partner)
         for p in range(2):
@@ -180,14 +180,13 @@
                 relay(1, 0).start()
             if t == NT - 1:
                 down_load(1).start()
+                with jax.named_scope('wait_f1'):
+                    arrived(source(1, c), 1)
+                    forward(1).start()
+                    relay(1, 1).start()
+                    for p in range(2):
+                        own(2, p).start()
             up_tile(0, t)
-    with jax.named_scope('wait_f1'):
-        arrived(source(1, c), 1)
-        forward(1).start()
-        relay(1, 1).start()
-        for p in range(2):
-            own(2, p).start()
-
     def chunk(k, carry):
         i = jnp.where(k == 1, 1, 5 - k)
         with jax.named_scope('wait_chunk'):
@@ -206,9 +205,12 @@
         for n in range(2):
             with jax.named_scope('down'):
                 down_tile(1, i, n)
-                for m in (2 * n, 2 * n + 1):
-                    for s in range(2):
-                        back_send(i, s, m).start()
+
+                @pl.when(k < 3)
+                def _():
+                    for m in BLOCK_MSGS[n]:
+                        for s in range(2):
+                            back_send(i, s, m).start()
             if n == 0:
                 with jax.named_scope('wait_direct'):
                     @pl.when(k == 1)
@@ -223,6 +225,12 @@
                         for p in range(2):
                             arrived(source(after, c), p)
                             relay(after, p).start()
+        @pl.when(k == 3)
+        def _():
+            for m in range(NM):
+                for s in range(2):
+                    back_send(i, s, m).start()
+
         return carry
 
     lax.fori_loop(1, 4, chunk, 0)
@@ -280,7 +288,7 @@
     def local_layer(x_loc, ids_loc, gates_loc, w_up, w_down):
         return pl.pallas_call(
             moe_kernel,
-            out_shape=jax.ShapeDtypeStruct((TOK, D), bf16),
+            out_shape=pltpu.VMEM((TOK, D), bf16),
             in_specs=[anyspace] * 5,
             out_specs=vmem,
             scratch_shapes=[

time: 56.4 us -> 53.8 us (0.954)
  Pallas kernels: 54.3 us -> 52.9 us
  local copies, waits for them, and re-layouts: 1.92 us -> 0.82 us
    pallas_call x1, Pallas kernels: 54.3 us -> 52.9 us  [local_layer(): pl.pallas_call(moe_kernel, out_shape=pltpu.VMEM((TOK, D), bf16), in_specs...]
    unnamed x1, local copies, waits for them, and re-layouts: 1.92 us -> 0.82 us
where the time goes in v4:
time: 53.8 us; the launch traced here: 53.7 us
  Pallas kernels  52.9 us (98%)
  local copies, waits for them, and re-layouts  0.82 us (2%)
    pallas_call x1, Pallas kernels, local_layer(): pl.pallas_call(moe_kernel, out_shape=pltpu.VMEM((TOK, D), bf16), in_specs...  52.9 us

profile of v4, /device:TPU:0, one launch (start us, length us, event | category | flops | bytes accessed | tf_op | source)
XLA Modules:
  0.0 53.7 jit_solution(3775302527650028174)
XLA Ops:
  0.0 52.9 %shard_map.55 = bf16[128,2304]{1,0:T(8,128)(2,1)S(1)} custom-call(bf16[128,2304]{1,0:T(8,128)(2,1)} %x_hbm.1, s32[2,128]{1,0:T(2,128)} %bitcast.2, f32[2,128]{1,0:T(2,128)} %bitcast.3, bf16[1,2304,5760]{2,1,0:T(8,128)(2,1)} %wu_hbm.1, bf16[1,5760,2304]{2,1,0:T(8,128)(2,1)} %wd_hbm.1), custom_call_target="tpu_custom_call" | custom-call | tf_op jit(solution)/shard_map/pallas_call | solution.py:289
  52.9 0.8 %copy.7 = bf16[128,2304]{1,0:T(8,128)(2,1)} copy(bf16[128,2304]{1,0:T(8,128)(2,1)S(1)} %shard_map.55) | data formatting | bytes 1179648

commit v5 on v4

v5 whole, which is shorter than its diff:
```python
import functools

import jax
import jax.numpy as jnp
from jax import lax
from jax.experimental import pallas as pl
from jax.experimental.pallas import tpu as pltpu
from jax.sharding import PartitionSpec as P

MESH = pl.DeviceIdType.MESH
TOK = 128
CAP = 64
EXP = 8
D = 2304
F = 5760
NU = 1024
NT = -(-F // NU)
F_TILE = 3
AHEAD = 2
DOWN = ((0, 512), (512, 512), (1024, 1280))
MSG = ((0, 512), (512, 512), (1024, 640), (1664, 384), (2048, 256))
BLOCK_MSGS = ((0,), (1,), (2, 3, 4))
NM = len(MSG)
HALF = TOK // 2
VMEM_LIMIT = 66400000


def remote(src, dst, send_sem, recv_sem, dev):
    return pltpu.make_async_remote_copy(src_ref=src, dst_ref=dst, send_sem=send_sem, recv_sem=recv_sem, device_id={'ep': dev}, device_id_type=MESH)


def moe_kernel(x_hbm, ids_hbm, gates_hbm, wu_hbm, wd_hbm, y_ref, ids_ref, gates_ref, wu, wd, xg, back, hid, xs, posg, post, send_x, send_m, send_b, rf, rx, rm, rb, sw, sl):
    me = lax.axis_index('ep')
    c = lax.rem(me, 2)
    x = lax.rem(me // 2, 2)
    y = me // 4

    def dev(yy, xx, cc):
        return yy * 4 + xx * 2 + cc

    partner = dev(y, x, 1 - c)
    first = dev(lax.rem(y + c, 2), lax.rem(x + 1 - c, 2), c)
    second = dev(lax.rem(y + 1 - c, 2), lax.rem(x + c, 2), c)
    def source(i, cc):
        lo, hi = lax.rem(i, 2), i // 2
        fx = lo * (1 - cc) + hi * cc
        fy = hi * (1 - cc) + lo * cc
        return dev(lax.rem(y + fy, 2), lax.rem(x + fx, 2), cc)

    barrier = pltpu.get_barrier_semaphore()
    for other in (partner, first, second):
        pl.semaphore_signal(barrier, inc=1, device_id={'ep': other}, device_id_type=MESH)
    ids_load = pltpu.make_async_copy(ids_hbm, ids_ref, sl.at[1])
    gates_load = pltpu.make_async_copy(gates_hbm, gates_ref, sl.at[2])
    ids_load.start()
    gates_load.start()
    own_load = pltpu.make_async_copy(x_hbm, xg.at[me], sl.at[0])
    own_load.start()

    def up_cols(t):
        return pl.ds(t * NU, min(NU, F - t * NU))

    def down_cols(n):
        return pl.ds(*DOWN[n])

    def msg_cols(m):
        return pl.ds(*MSG[m])

    def up_load(t):
        return pltpu.make_async_copy(wu_hbm.at[0, :, up_cols(t)], wu.at[:, up_cols(t)], sw.at[t])

    def down_load(n):
        cols = pl.ds(*((0, 1024), (1024, 1280))[n])
        return pltpu.make_async_copy(wd_hbm.at[0, :, cols], wd.at[:, cols], sw.at[NT + n])

    with jax.named_scope('own_load'):
        own_load.wait()
    for t in range(AHEAD):
        up_load(t).start()
    with jax.named_scope('barrier'):
        pl.semaphore_wait(barrier, 3)

    def half(s, p, recv_sem, to):
        rows = pl.ds(p * HALF, HALF)
        return remote(xg.at[s, rows], xg.at[s, rows], send_x, recv_sem, to)

    def block(s, to):
        return remote(xg.at[s], xg.at[s], send_x, rx.at[s], to)

    def arrived(s):
        block(s, partner).wait_recv()

    def meta_arrived(s):
        meta(s, partner).wait_recv()

    def meta(s, to):
        return remote(posg.at[s], posg.at[s], send_m, rm.at[s], to)

    def back_send(i, s, m):
        return remote(xg.at[source(i, 1 - c), pl.ds(s * CAP, CAP), msg_cols(m)], back.at[me, :, msg_cols(m)], send_b, rb.at[m], source(i, s))

    def back_partner(m):
        return remote(xg.at[partner, pl.ds(pl.multiple_of((1 - c) * CAP, CAP), CAP), msg_cols(m)], back.at[me, :, msg_cols(m)], send_b, rb.at[m], partner)

    def gather(i, s):
        s_id = source(i, s)
        where = posg[s_id, pl.ds(me, 1), :]
        rank_row = lax.broadcasted_iota(jnp.int32, (CAP, TOK), 0).astype(jnp.float32)
        pick = jnp.where(rank_row == where, 1.0, 0.0).astype(jnp.bfloat16)
        xs[s * CAP:(s + 1) * CAP, :] = jnp.dot(pick, xg[s_id], preferred_element_type=jnp.float32).astype(jnp.bfloat16)

    def up_tile(h, t):
        z = jnp.dot(xs[...], wu[:, up_cols(t)], preferred_element_type=jnp.float32)
        hid[h, :, up_cols(t)] = jax.nn.gelu(z, approximate=True).astype(jnp.bfloat16)

    def down_tile(h, i, n):
        xg[source(i, 1 - c), :, down_cols(n)] = jnp.dot(hid[h], wd[:, down_cols(n)], preferred_element_type=jnp.float32).astype(jnp.bfloat16)

    def own_down(n):
        down_tile(0, 0, n)
        for m in BLOCK_MSGS[n]:
            back_partner(m).start()
        back[me, :, down_cols(n)] = xg[partner, pl.ds(pl.multiple_of(c * CAP, CAP), CAP), down_cols(n)]

    half(me, 0, rf, first).start()
    block(me, partner).start()
    for t in range(AHEAD, 4):
        up_load(t).start()
    ids_load.wait()
    gates_load.wait()
    lane = lax.broadcasted_iota(jnp.int32, (TOK, TOK), 1)
    row = lax.broadcasted_iota(jnp.int32, (TOK, TOK), 0)
    expert_row = lax.broadcasted_iota(jnp.int32, (EXP, TOK), 0)
    hit = (ids_ref[0:1, :] == expert_row) | (ids_ref[1:2, :] == expert_row)
    upper = jnp.where(row < lane, 1.0, 0.0).astype(jnp.bfloat16)
    rank = jnp.dot(jnp.where(hit, 1.0, 0.0).astype(jnp.bfloat16), upper, preferred_element_type=jnp.float32)
    slots = jnp.where(hit, rank, -1.0)
    posg[me] = slots
    pad = jnp.zeros((TOK - EXP - 4, TOK), jnp.float32)
    post[...] = jnp.concatenate([slots, ids_ref[...].astype(jnp.float32), gates_ref[...], pad], axis=0).T
    for to in (first, partner, second):
        meta(me, to).start()
    half(me, 1, rx.at[me], first).start()
    near = source(1, c)
    with jax.named_scope('wait_partner'):
        meta_arrived(partner)
        arrived(partner)
    with jax.named_scope('up0'):
        gather(0, 0)
        gather(0, 1)
        for t in range(NT):
            up_load(t).wait()
            if t < 2:
                up_load(4 + t).start()
            if t == 2:
                down_load(0).start()
            if t == F_TILE:
                with jax.named_scope('wait_f0'):
                    meta_arrived(near)
                    half(near, 0, rf, partner).wait_recv()
                for to in (second, partner):
                    meta(near, to).start()
                    half(near, 0, rx.at[near], to).start()
            if t == NT - 1:
                down_load(1).start()
                with jax.named_scope('wait_f1'):
                    half(near, 1, rx.at[near], partner).wait_recv()
                    for to in (second, partner):
                        half(near, 1, rx.at[near], to).start()
                    block(me, second).start()
            up_tile(0, t)

    def chunk(k, carry):
        i = jnp.where(k == 1, 1, 5 - k)
        with jax.named_scope('wait_chunk'):
            meta_arrived(source(i, 1 - c))
            arrived(source(i, 1 - c))
        with jax.named_scope('up'):
            gather(i, 0)
            gather(i, 1)
            for t in range(NT):
                up_tile(1, t)

        @pl.when(k == 1)
        def _():
            down_load(0).wait()

        for n in range(len(DOWN)):
            with jax.named_scope('down'):
                down_tile(1, i, n)

                @pl.when(k < 3)
                def _():
                    for m in BLOCK_MSGS[n]:
                        for s in range(2):
                            back_send(i, s, m).start()
            if n == 0:
                with jax.named_scope('wait_direct'):
                    @pl.when(k == 1)
                    def _():
                        down_load(1).wait()

                    @pl.when(k < 3)
                    def _():
                        after = source(4 - k, c)
                        meta_arrived(after)
                        arrived(after)
                        meta(after, partner).start()
                        block(after, partner).start()
        @pl.when(k == 3)
        def _():
            for m in range(NM):
                for s in range(2):
                    back_send(i, s, m).start()

        return carry

    lax.fori_loop(1, 4, chunk, 0)
    with jax.named_scope('own_down'):
        for n in range(len(DOWN)):
            own_down(n)

    cols8 = post[...]
    low = lane < CAP
    parts = []
    for k in range(EXP // 2):
        at = jnp.where(low, cols8[:, 2 * k:2 * k + 1], cols8[:, 2 * k + 1:2 * k + 2])
        here = at == (lane - jnp.where(low, 0, CAP)).astype(jnp.float32)
        parts.append((here, (2 * k + jnp.where(low, 0, 1)).astype(jnp.float32)))
    choice = [cols8[:, EXP + j:EXP + j + 1] for j in range(2)]
    picks = jnp.concatenate([jnp.concatenate([jnp.where(here & (expert == idj), 1.0, 0.0).astype(jnp.bfloat16) for here, expert in parts], axis=1) for idj in choice], axis=0)
    g0 = cols8[:, EXP + 2:EXP + 3]
    g1 = cols8[:, EXP + 3:EXP + 4]

    for m in range(NM):
        cols = msg_cols(m)
        with jax.named_scope('wait_back'):
            seven = back.at[pl.ds(0, EXP - 1), :, cols]
            remote(seven, seven, send_b, rb.at[m], partner).wait_recv()
        with jax.named_scope('combine'):
            rows = back[:, :, cols].reshape(EXP * CAP, MSG[m][1])
            got = jnp.dot(picks, rows, preferred_element_type=jnp.float32)
            y_ref[:, cols] = (g0 * got[:TOK] + g1 * got[TOK:]).astype(jnp.bfloat16)

    for sent, sem in ((xg, send_x), (posg, send_m), (back, send_b)):
        seven = sent.at[pl.ds(0, EXP - 1)]
        remote(seven, seven, sem, rf, partner).wait_send()


def solution(mesh):
    token_spec = P(('dp', 'ep'), None)
    expert_spec = P('ep', None, None)
    vmem = pl.BlockSpec(memory_space=pltpu.VMEM)
    anyspace = pl.BlockSpec(memory_space=pl.ANY)
    bf16, f32 = jnp.bfloat16, jnp.float32

    def local_layer(x_loc, ids_loc, gates_loc, w_up, w_down):
        return pl.pallas_call(
            moe_kernel,
            out_shape=pltpu.VMEM((TOK, D), bf16),
            in_specs=[anyspace] * 5,
            out_specs=vmem,
            scratch_shapes=[
                pltpu.VMEM((2, TOK), jnp.int32),
                pltpu.VMEM((2, TOK), f32),
                pltpu.VMEM((D, F), bf16),
                pltpu.VMEM((F, D), bf16),
                pltpu.VMEM((EXP, TOK, D), bf16),
                pltpu.VMEM((EXP, CAP, D), bf16),
                pltpu.VMEM((2, TOK, F), bf16),
                pltpu.VMEM((TOK, D), bf16),
                pltpu.VMEM((EXP, EXP, TOK), f32),
                pltpu.VMEM((TOK, TOK), f32),
                pltpu.SemaphoreType.DMA,
                pltpu.SemaphoreType.DMA,
                pltpu.SemaphoreType.DMA,
                pltpu.SemaphoreType.DMA,
                pltpu.SemaphoreType.DMA((EXP,)),
                pltpu.SemaphoreType.DMA((EXP,)),
                pltpu.SemaphoreType.DMA((NM,)),
                pltpu.SemaphoreType.DMA((NT + 2,)),
                pltpu.SemaphoreType.DMA((3,)),
            ],
            compiler_params=pltpu.CompilerParams(vmem_limit_bytes=VMEM_LIMIT, collective_id=0, has_side_effects=True),
        )(x_loc, ids_loc.T, gates_loc.T, w_up, w_down)

    return jax.shard_map(local_layer, mesh=mesh, in_specs=(token_spec, token_spec, token_spec, expert_spec, expert_spec), out_specs=token_spec, check_vma=False)
```

time: 53.8 us -> 52.7 us (0.980)
  Pallas kernels: 52.9 us -> 51.7 us
    pallas_call x1, Pallas kernels: 52.9 us -> 51.7 us  [local_layer(): pl.pallas_call(moe_kernel, out_shape=pltpu.VMEM((TOK, D), bf16), in_specs...]
where the time goes in v5:
time: 52.7 us; the launch traced here: 52.6 us
  Pallas kernels  51.7 us (98%)
  local copies, waits for them, and re-layouts  0.82 us (2%)
    pallas_call x1, Pallas kernels, local_layer(): pl.pallas_call(moe_kernel, out_shape=pltpu.VMEM((TOK, D), bf16), in_specs...  51.7 us

profile of v5, /device:TPU:0, one launch (start us, length us, event | category | flops | bytes accessed | tf_op | source)
XLA Modules:
  0.0 52.6 jit_solution(5291132232310497965)
XLA Ops:
  0.0 51.7 %shard_map.55 = bf16[128,2304]{1,0:T(8,128)(2,1)S(1)} custom-call(bf16[128,2304]{1,0:T(8,128)(2,1)} %x_hbm.1, s32[2,128]{1,0:T(2,128)} %bitcast.2, f32[2,128]{1,0:T(2,128)} %bitcast.3, bf16[1,2304,5760]{2,1,0:T(8,128)(2,1)} %wu_hbm.1, bf16[1,5760,2304]{2,1,0:T(8,128)(2,1)} %wd_hbm.1), custom_call_target="tpu_custom_call" | custom-call | tf_op jit(solution)/shard_map/pallas_call | solution.py:258
  51.7 0.8 %copy.7 = bf16[128,2304]{1,0:T(8,128)(2,1)} copy(bf16[128,2304]{1,0:T(8,128)(2,1)S(1)} %shard_map.55) | data formatting | bytes 1179648

commit v6 on v5

--- a/solution.py
+++ b/solution.py
@@ -39,14 +39,16 @@
         return yy * 4 + xx * 2 + cc
 
     partner = dev(y, x, 1 - c)
-    first = dev(lax.rem(y + c, 2), lax.rem(x + 1 - c, 2), c)
-    second = dev(lax.rem(y + 1 - c, 2), lax.rem(x + c, 2), c)
+    first = dev(lax.rem(y + 1 - c, 2), lax.rem(x + c, 2), c)
+    second = dev(lax.rem(y + c, 2), lax.rem(x + 1 - c, 2), c)
     def source(i, cc):
         lo, hi = lax.rem(i, 2), i // 2
-        fx = lo * (1 - cc) + hi * cc
-        fy = hi * (1 - cc) + lo * cc
+        fy = lo * (1 - cc) + hi * cc
+        fx = hi * (1 - cc) + lo * cc
         return dev(lax.rem(y + fy, 2), lax.rem(x + fx, 2), cc)
 
+    own_load = pltpu.make_async_copy(x_hbm, xg.at[me], sl.at[0])
+    own_load.start()
     barrier = pltpu.get_barrier_semaphore()
     for other in (partner, first, second):
         pl.semaphore_signal(barrier, inc=1, device_id={'ep': other}, device_id_type=MESH)
@@ -54,9 +56,6 @@
     gates_load = pltpu.make_async_copy(gates_hbm, gates_ref, sl.at[2])
     ids_load.start()
     gates_load.start()
-    own_load = pltpu.make_async_copy(x_hbm, xg.at[me], sl.at[0])
-    own_load.start()
-
     def up_cols(t):
         return pl.ds(t * NU, min(NU, F - t * NU))
 

time: 52.7 us -> 52.2 us (level)
  no operation moved by 1% of the time
where the time goes in v6:
time: 52.2 us; the launch traced here: 52.1 us
  Pallas kernels  51.3 us (98%)
  local copies, waits for them, and re-layouts  0.82 us (2%)
    pallas_call x1, Pallas kernels, local_layer(): pl.pallas_call(moe_kernel, out_shape=pltpu.VMEM((TOK, D), bf16), in_specs...  51.3 us

profile of v6, /device:TPU:0, one launch (start us, length us, event | category | flops | bytes accessed | tf_op | source)
XLA Modules:
  0.0 52.1 jit_solution(15503360372482145946)
XLA Ops:
  0.0 51.3 %shard_map.55 = bf16[128,2304]{1,0:T(8,128)(2,1)S(1)} custom-call(bf16[128,2304]{1,0:T(8,128)(2,1)} %x_hbm.1, s32[2,128]{1,0:T(2,128)} %bitcast.2, f32[2,128]{1,0:T(2,128)} %bitcast.3, bf16[1,2304,5760]{2,1,0:T(8,128)(2,1)} %wu_hbm.1, bf16[1,5760,2304]{2,1,0:T(8,128)(2,1)} %wd_hbm.1), custom_call_target="tpu_custom_call" | custom-call | tf_op jit(solution)/shard_map/pallas_call | solution.py:257
  51.3 0.8 %copy.7 = bf16[128,2304]{1,0:T(8,128)(2,1)} copy(bf16[128,2304]{1,0:T(8,128)(2,1)S(1)} %shard_map.55) | data formatting | bytes 1179648

commit v7 on v6

--- a/solution.py
+++ b/solution.py
@@ -29,7 +29,7 @@
     return pltpu.make_async_remote_copy(src_ref=src, dst_ref=dst, send_sem=send_sem, recv_sem=recv_sem, device_id={'ep': dev}, device_id_type=MESH)
 
 
-def moe_kernel(x_hbm, ids_hbm, gates_hbm, wu_hbm, wd_hbm, y_ref, ids_ref, gates_ref, wu, wd, xg, back, hid, xs, posg, post, send_x, send_m, send_b, rf, rx, rm, rb, sw, sl):
+def moe_kernel(x_hbm, ids_hbm, gates_hbm, wu_hbm, wd_hbm, y_ref, ids_ref, gates_ref, wu, wd, xg, back, hid, xs, posg, post, send_x, send_m, send_b, rf, rx, rm, rb, sw, sl, ready):
     me = lax.axis_index('ep')
     c = lax.rem(me, 2)
     x = lax.rem(me // 2, 2)
@@ -50,7 +50,7 @@
     own_load = pltpu.make_async_copy(x_hbm, xg.at[me], sl.at[0])
     own_load.start()
     barrier = pltpu.get_barrier_semaphore()
-    for other in (partner, first, second):
+    for other in (partner, first):
         pl.semaphore_signal(barrier, inc=1, device_id={'ep': other}, device_id_type=MESH)
     ids_load = pltpu.make_async_copy(ids_hbm, ids_ref, sl.at[1])
     gates_load = pltpu.make_async_copy(gates_hbm, gates_ref, sl.at[2])
@@ -77,7 +77,7 @@
     for t in range(AHEAD):
         up_load(t).start()
     with jax.named_scope('barrier'):
-        pl.semaphore_wait(barrier, 3)
+        pl.semaphore_wait(barrier, 2)
 
     def half(s, p, recv_sem, to):
         rows = pl.ds(p * HALF, HALF)
@@ -137,7 +137,7 @@
     posg[me] = slots
     pad = jnp.zeros((TOK - EXP - 4, TOK), jnp.float32)
     post[...] = jnp.concatenate([slots, ids_ref[...].astype(jnp.float32), gates_ref[...], pad], axis=0).T
-    for to in (first, partner, second):
+    for to in (first, partner):
         meta(me, to).start()
     half(me, 1, rx.at[me], first).start()
     near = source(1, c)
@@ -157,6 +157,9 @@
                 with jax.named_scope('wait_f0'):
                     meta_arrived(near)
                     half(near, 0, rf, partner).wait_recv()
+                pl.semaphore_signal(ready, inc=1, device_id={'ep': partner}, device_id_type=MESH)
+                pl.semaphore_wait(ready, 1)
+                meta(me, second).start()
                 for to in (second, partner):
                     meta(near, to).start()
                     half(near, 0, rx.at[near], to).start()
@@ -279,6 +282,7 @@
                 pltpu.SemaphoreType.DMA((NM,)),
                 pltpu.SemaphoreType.DMA((NT + 2,)),
                 pltpu.SemaphoreType.DMA((3,)),
+                pltpu.SemaphoreType.REGULAR,
             ],
             compiler_params=pltpu.CompilerParams(vmem_limit_bytes=VMEM_LIMIT, collective_id=0, has_side_effects=True),
         )(x_loc, ids_loc.T, gates_loc.T, w_up, w_down)

time: 52.2 us -> 52 us (level)
  no operation moved by 1% of the time
where the time goes in v7:
time: 52 us; the launch traced here: 51.9 us
  Pallas kernels  51.1 us (98%)
  local copies, waits for them, and re-layouts  0.82 us (2%)
    pallas_call x1, Pallas kernels, local_layer(): pl.pallas_call(moe_kernel, out_shape=pltpu.VMEM((TOK, D), bf16), in_specs...  51.1 us

profile of v7, /device:TPU:0, one launch (start us, length us, event | category | flops | bytes accessed | tf_op | source)
XLA Modules:
  0.0 51.9 jit_solution(14644620920760169330)
XLA Ops:
  0.0 51.1 %shard_map.55 = bf16[128,2304]{1,0:T(8,128)(2,1)S(1)} custom-call(bf16[128,2304]{1,0:T(8,128)(2,1)} %x_hbm.1, s32[2,128]{1,0:T(2,128)} %bitcast.2, f32[2,128]{1,0:T(2,128)} %bitcast.3, bf16[1,2304,5760]{2,1,0:T(8,128)(2,1)} %wu_hbm.1, bf16[1,5760,2304]{2,1,0:T(8,128)(2,1)} %wd_hbm.1), custom_call_target="tpu_custom_call" | custom-call | tf_op jit(solution)/shard_map/pallas_call | solution.py:260
  51.1 0.8 %copy.7 = bf16[128,2304]{1,0:T(8,128)(2,1)} copy(bf16[128,2304]{1,0:T(8,128)(2,1)S(1)} %shard_map.55) | data formatting | bytes 1179648

commit v8 on v7

--- a/solution.py
+++ b/solution.py
@@ -47,8 +47,9 @@
         fx = hi * (1 - cc) + lo * cc
         return dev(lax.rem(y + fy, 2), lax.rem(x + fx, 2), cc)
 
-    own_load = pltpu.make_async_copy(x_hbm, xg.at[me], sl.at[0])
-    own_load.start()
+    own_loads = [pltpu.make_async_copy(x_hbm.at[pl.ds(p * HALF, HALF)], xg.at[me, pl.ds(p * HALF, HALF)], sl.at[3 * p]) for p in range(2)]
+    for own_load in own_loads:
+        own_load.start()
     barrier = pltpu.get_barrier_semaphore()
     for other in (partner, first):
         pl.semaphore_signal(barrier, inc=1, device_id={'ep': other}, device_id_type=MESH)
@@ -73,7 +74,7 @@
         return pltpu.make_async_copy(wd_hbm.at[0, :, cols], wd.at[:, cols], sw.at[NT + n])
 
     with jax.named_scope('own_load'):
-        own_load.wait()
+        own_loads[0].wait()
     for t in range(AHEAD):
         up_load(t).start()
     with jax.named_scope('barrier'):
@@ -122,6 +123,7 @@
         back[me, :, down_cols(n)] = xg[partner, pl.ds(pl.multiple_of(c * CAP, CAP), CAP), down_cols(n)]
 
     half(me, 0, rf, first).start()
+    own_loads[1].wait()
     block(me, partner).start()
     for t in range(AHEAD, 4):
         up_load(t).start()
@@ -281,7 +283,7 @@
                 pltpu.SemaphoreType.DMA((EXP,)),
                 pltpu.SemaphoreType.DMA((NM,)),
                 pltpu.SemaphoreType.DMA((NT + 2,)),
-                pltpu.SemaphoreType.DMA((3,)),
+                pltpu.SemaphoreType.DMA((4,)),
                 pltpu.SemaphoreType.REGULAR,
             ],
             compiler_params=pltpu.CompilerParams(vmem_limit_bytes=VMEM_LIMIT, collective_id=0, has_side_effects=True),

time: 52 us -> 51.9 us (level)
  no operation moved by 1% of the time
where the time goes in v8:
time: 51.9 us; the launch traced here: 51.8 us
  Pallas kernels  51 us (98%)
  local copies, waits for them, and re-layouts  0.82 us (2%)
    pallas_call x1, Pallas kernels, local_layer(): pl.pallas_call(moe_kernel, out_shape=pltpu.VMEM((TOK, D), bf16), in_specs...  51 us

profile of v8, /device:TPU:0, one launch (start us, length us, event | category | flops | bytes accessed | tf_op | source)
XLA Modules:
  0.0 51.8 jit_solution(12766109421735734605)
XLA Ops:
  0.0 51.0 %shard_map.55 = bf16[128,2304]{1,0:T(8,128)(2,1)S(1)} custom-call(bf16[128,2304]{1,0:T(8,128)(2,1)} %x_hbm.1, s32[2,128]{1,0:T(2,128)} %bitcast.2, f32[2,128]{1,0:T(2,128)} %bitcast.3, bf16[1,2304,5760]{2,1,0:T(8,128)(2,1)} %wu_hbm.1, bf16[1,5760,2304]{2,1,0:T(8,128)(2,1)} %wd_hbm.1), custom_call_target="tpu_custom_call" | custom-call | tf_op jit(solution)/shard_map/pallas_call | solution.py:262
  51.0 0.8 %copy.7 = bf16[128,2304]{1,0:T(8,128)(2,1)} copy(bf16[128,2304]{1,0:T(8,128)(2,1)S(1)} %shard_map.55) | data formatting | bytes 1179648

commit v9 on v8

--- a/solution.py
+++ b/solution.py
@@ -18,8 +18,8 @@
 F_TILE = 3
 AHEAD = 2
 DOWN = ((0, 512), (512, 512), (1024, 1280))
-MSG = ((0, 512), (512, 512), (1024, 640), (1664, 384), (2048, 256))
-BLOCK_MSGS = ((0,), (1,), (2, 3, 4))
+MSG = ((0, 512), (512, 512), (1024, 640), (1664, 256), (1920, 256), (2176, 128))
+BLOCK_MSGS = ((0,), (1,), (2, 3, 4, 5))
 NM = len(MSG)
 HALF = TOK // 2
 VMEM_LIMIT = 66400000

time: 51.9 us -> 52.1 us (level)
  no operation moved by 1% of the time
where the time goes in v9:
time: 52.1 us; the launch traced here: 52 us
  Pallas kernels  51.1 us (98%)
  local copies, waits for them, and re-layouts  0.82 us (2%)
    pallas_call x1, Pallas kernels, local_layer(): pl.pallas_call(moe_kernel, out_shape=pltpu.VMEM((TOK, D), bf16), in_specs...  51.1 us

profile of v9, /device:TPU:0, one launch (start us, length us, event | category | flops | bytes accessed | tf_op | source)
XLA Modules:
  0.0 52.0 jit_solution(11670838422985732585)
XLA Ops:
  0.0 51.1 %shard_map.55 = bf16[128,2304]{1,0:T(8,128)(2,1)S(1)} custom-call(bf16[128,2304]{1,0:T(8,128)(2,1)} %x_hbm.1, s32[2,128]{1,0:T(2,128)} %bitcast.2, f32[2,128]{1,0:T(2,128)} %bitcast.3, bf16[1,2304,5760]{2,1,0:T(8,128)(2,1)} %wu_hbm.1, bf16[1,5760,2304]{2,1,0:T(8,128)(2,1)} %wd_hbm.1), custom_call_target="tpu_custom_call" | custom-call | tf_op jit(solution)/shard_map/pallas_call | solution.py:262
  51.1 0.8 %copy.7 = bf16[128,2304]{1,0:T(8,128)(2,1)} copy(bf16[128,2304]{1,0:T(8,128)(2,1)S(1)} %shard_map.55) | data formatting | bytes 1179648
